TPU v7x, 256 devices: a whole 4x4x8 slice. The times are simulated.
256 devices in a mesh: space: 8 (over y_hi, x), vel: 32 (over z, y_lo, core).
Axes of the slice: x: 4, y: 4 (y_hi: 2, y_lo: 2; y = y_hi * 2 + y_lo), z: 8, core: 2. Of those that a mesh axis runs over, the one named last changes fastest.
Arguments:
- distribution: float32 [8, 16, 16, 32768], P('space', None, None, 'vel'), may hold values from 0.003 to 450, as said below
- inflow: float32 [2, 16, 16, 32768], P(None, None, None, 'vel'), may hold values from 0.3 to 3
- wall_temp: float32 [2, 16, 16], replicated, may hold values from 0.5 to 4
- face_type: int32 [2, 16, 16], replicated, may hold values from 0 to 2
Outputs:
- updated: float32 [8, 16, 16, 32768], P('space', None, None, 'vel')
- fields: float32 [8, 8, 16, 16], P(None, 'space')
Inputs may be any that keep to these rules, and one draw needn't show every extreme that they name: `distribution`: every entry is positive.
All inputs are finite; a program needn't handle non-finite values.
Results may differ from a plain program's by a relative error of at most 0.0003.
Values sent between devices are 32-bit elements; how exact they have to be, the bound alone decides.
No kernel may reach another device: no remote copies, remote signals or barrier semaphores. Data moves between devices by JAX's collectives and lax.ppermute only.
A program may use at most 64 MiB of HBM per device.

v0:
```python
import jax
import jax.numpy as jnp
from jax import lax
from jax.sharding import PartitionSpec as P

NVX = 32
NVY = 32
NVZ = 32
OUTER = 2
INNER = 3
box_volume = 512.0
speed_top = 4.0
courant = 0.08
impact_rate_field = 0.8
shakhov_factor = 1.0 / 3.0


def padded_2(cells, sides, width):
    for axis, dim in sides:
        count = lax.axis_size(axis)
        ends = count - 1
        head = lax.slice_in_dim(cells, 0, width, axis=dim)
        tail = lax.slice_in_dim(cells, cells.shape[dim] - width, cells.shape[dim], axis=dim)
        cells = jnp.concatenate(
            [
                lax.ppermute(tail, axis, [(i, (i + 1) % count) for i in range(ends)]),
                cells,
                lax.ppermute(head, axis, [((i + 1) % count, i) for i in range(ends)]),
            ],
            axis=dim,
        )
    return cells


def velocity_table(count_x, count_y, count_z, shards):
    velocity_total = count_x * count_y * count_z
    velocity_index = jnp.arange(velocity_total, dtype=jnp.int32)
    per_shard = velocity_total // shards
    halves = per_shard // 2
    owner_shard = velocity_index // per_shard
    within = velocity_index % per_shard
    upper_half = within // halves
    ranked = owner_shard * halves + within % halves
    layer_size = count_y * count_z
    level_x = ranked // layer_size
    remain = ranked % layer_size
    across_y = remain // count_z
    across_z = remain % count_z
    sign_x = 2.0 * upper_half.astype(jnp.float32) - 1.0
    speed_x = sign_x * (level_x.astype(jnp.float32) + 0.5) * (2.0 * speed_top / count_x)
    speed_y = (across_y.astype(jnp.float32) + 0.5) * (2.0 * speed_top / count_y) - speed_top
    speed_z = (across_z.astype(jnp.float32) + 0.5) * (2.0 * speed_top / count_z) - speed_top
    return (speed_x, speed_y, speed_z)


def wall_shape(wall_temp, speed_sq):
    temp_cell = wall_temp[..., None]
    return box_volume * jnp.exp(-speed_sq / (2.0 * temp_cell)) / (2.0 * jnp.pi * temp_cell) ** 1.5


def boundary_planes(edge_planes, leaving, entering, wall_profile, inflow, face_type):
    wall_planes = (leaving / entering)[..., None] * wall_profile
    face_kind = face_type[..., None]
    return jnp.where(face_kind == 0, wall_planes, jnp.where(face_kind == 1, inflow, edge_planes))


def transport(current, west_plane, east_plane, speed_x, speed_y, speed_z):
    west_cells = jnp.concatenate([west_plane[None], current[:-1]], 0)
    east_cells = jnp.concatenate([current[1:], east_plane[None]], 0)
    flux_sum = jnp.maximum(speed_x, 0.0) * (current - west_cells) + jnp.minimum(speed_x, 0.0) * (
        east_cells - current
    )
    flux_sum = (
        flux_sum
        + jnp.maximum(speed_y, 0.0) * (current - jnp.roll(current, 1, 1))
        + jnp.minimum(speed_y, 0.0) * (jnp.roll(current, -1, 1) - current)
    )
    flux_sum = (
        flux_sum
        + jnp.maximum(speed_z, 0.0) * (current - jnp.roll(current, 1, 2))
        + jnp.minimum(speed_z, 0.0) * (jnp.roll(current, -1, 2) - current)
    )
    return current - courant * flux_sum


def macro_fields(
    particle_concentration,
    mean_motion_first_axis,
    mean_motion_second_axis,
    mean_motion_third_axis,
    maxwellian_width,
    energy_current_first,
    energy_current_second,
    energy_current_third,
):
    kinetic_warmth = maxwellian_width / (3.0 * particle_concentration)
    decay_rate_toward_target = (
        impact_rate_field * particle_concentration * jnp.exp(0.19 * jnp.log(kinetic_warmth))
    )
    return jnp.stack(
        [
            particle_concentration,
            mean_motion_first_axis,
            mean_motion_second_axis,
            mean_motion_third_axis,
            kinetic_warmth,
            energy_current_first,
            energy_current_second,
            energy_current_third,
            decay_rate_toward_target,
        ]
    )


def shakhov(params, speed_x, speed_y, speed_z):
    particle_concentration = params[0][..., None]
    peculiar_x = speed_x - params[1][..., None]
    peculiar_y = speed_y - params[2][..., None]
    peculiar_z = speed_z - params[3][..., None]
    temp_cell = params[4][..., None]
    speed_sq = peculiar_x * peculiar_x + peculiar_y * peculiar_y + peculiar_z * peculiar_z
    maxwell = (
        particle_concentration
        * box_volume
        * jnp.exp(-speed_sq / (2.0 * temp_cell))
        / (2.0 * jnp.pi * temp_cell) ** 1.5
    )
    heat_term = (
        params[5][..., None] * peculiar_x
        + params[6][..., None] * peculiar_y
        + params[7][..., None] * peculiar_z
    ) / (5.0 * particle_concentration * temp_cell * temp_cell)
    return maxwell * (1.0 + shakhov_factor * heat_term * (speed_sq / temp_cell - 5.0))


def relaxation(read, params, speed_x, speed_y, speed_z):
    decay_rate_toward_target = params[8][..., None]
    return (read + decay_rate_toward_target * shakhov(params, speed_x, speed_y, speed_z)) / (
        1.0 + decay_rate_toward_target
    )


def moment_fields(current, moment_table, speed_x, speed_y, speed_z, velocity_total):
    cell_count = current.shape[0] * current.shape[1] * current.shape[2]
    flattened = current.reshape(cell_count, current.shape[3])
    partial_value = jnp.einsum(
        "cv,vk->kc", flattened, moment_table[:, :4], precision=lax.Precision.HIGHEST
    )
    first_sum = lax.psum(partial_value, "vel") / velocity_total
    particle_concentration = first_sum[0]
    mean_motion_first_axis = first_sum[1] / particle_concentration
    mean_motion_second_axis = first_sum[2] / particle_concentration
    mean_motion_third_axis = first_sum[3] / particle_concentration
    peculiar_x = speed_x[None, :] - mean_motion_first_axis[:, None]
    peculiar_y = speed_y[None, :] - mean_motion_second_axis[:, None]
    peculiar_z = speed_z[None, :] - mean_motion_third_axis[:, None]
    speed_sq = peculiar_x * peculiar_x + peculiar_y * peculiar_y + peculiar_z * peculiar_z
    weighted = flattened * speed_sq
    second = jnp.stack(
        [
            jnp.sum(weighted, 1),
            0.5 * jnp.sum(weighted * peculiar_x, 1),
            0.5 * jnp.sum(weighted * peculiar_y, 1),
            0.5 * jnp.sum(weighted * peculiar_z, 1),
        ]
    )
    second = lax.psum(second, "vel") / velocity_total
    params = macro_fields(
        particle_concentration,
        mean_motion_first_axis,
        mean_motion_second_axis,
        mean_motion_third_axis,
        second[0],
        second[1],
        second[2],
        second[3],
    )
    return params.reshape((9,) + current.shape[:3])


def body(distribution, inflow, wall_temp, face_type):
    velocity_total = NVX * NVY * NVZ
    local_count = distribution.shape[3]
    full_x, full_y, full_z = velocity_table(NVX, NVY, NVZ, lax.axis_size("vel"))
    offset = lax.axis_index("vel") * local_count
    speed_x = lax.dynamic_slice_in_dim(full_x, offset, local_count)
    speed_y = lax.dynamic_slice_in_dim(full_y, offset, local_count)
    speed_z = lax.dynamic_slice_in_dim(full_z, offset, local_count)
    speed_sq = speed_x * speed_x + speed_y * speed_y + speed_z * speed_z
    moment_table = jnp.stack(
        [
            jnp.ones_like(speed_x),
            speed_x,
            speed_y,
            speed_z,
            speed_x * speed_x,
            speed_y * speed_y,
            speed_z * speed_z,
            speed_x * speed_y,
            speed_x * speed_z,
            speed_y * speed_z,
            0.5 * speed_x * speed_sq,
            0.5 * speed_y * speed_sq,
            0.5 * speed_z * speed_sq,
        ],
        1,
    )
    lowest_slab = lax.axis_index("space") == 0
    highest_slab = lax.axis_index("space") == lax.axis_size("space") - 1
    wall_profile = wall_shape(wall_temp, speed_sq)
    outward = jnp.stack([-speed_x, speed_x])[:, None, None, :]
    entering_part = jnp.sum(wall_profile * jnp.maximum(-outward, 0.0), -1)
    current = distribution
    params = None
    for outer_turn in range(OUTER):
        edge_planes = jnp.stack([current[0], current[-1]])
        leaving_part = jnp.sum(edge_planes * jnp.maximum(outward, 0.0), -1)
        leaving, entering = lax.psum((leaving_part, entering_part), "vel")
        ghost_planes = boundary_planes(
            edge_planes, leaving, entering, wall_profile, inflow, face_type
        )
        padded = padded_2(current, (("space", 0),), 1)
        west_plane = jnp.where(lowest_slab, ghost_planes[0], padded[0])
        east_plane = jnp.where(highest_slab, ghost_planes[1], padded[-1])
        read = transport(current, west_plane, east_plane, speed_x, speed_y, speed_z)
        current = read
        for inner_turn in range(INNER):
            params = moment_fields(current, moment_table, speed_x, speed_y, speed_z, velocity_total)
            current = relaxation(read, params, speed_x, speed_y, speed_z)
    return (current, params[:8])


def solution(mesh):
    in_specs = (P("space", None, None, "vel"), P(None, None, None, "vel"), P(), P())
    out_specs = (P("space", None, None, "vel"), P(None, "space", None, None))
    return jax.shard_map(body, mesh=mesh, in_specs=in_specs, out_specs=out_specs, check_vma=False)
```

profile of v0, /device:TPU:23, one launch (start us, length us, event | category | flops | bytes accessed | tf_op | source)
XLA Modules:
  0.0 943.6 jit_solution(8310820581644365251)
XLA Ops:
  0.6 1.4 collective-permute-start
  2.1 5.0 collective-permute-start.1
  7.1 0.8 negate_select_fusion
  7.8 0.8 negate_select_fusion.1
  8.6 0.7 negate_select_fusion.3
  9.3 0.7 negate_select_fusion.6
  10.0 0.7 broadcast_compare_fusion
  10.7 0.7 broadcast_compare_fusion.1
  11.4 0.6 fusion.186
  12.1 0.7 fusion.187
  12.8 0.7 sign_compare_fusion
  13.5 0.7 sign_compare_fusion.1
  14.1 2.3 constant_dynamic-update-slice_fusion.1
  16.5 1.2 fusion.249
  17.8 1.1 constant_dynamic-update-slice_fusion
  19.5 0.8 broadcast_maximum_fusion.2
  20.4 0.7 multiply_reduce_fusion
  21.0 1.8 multiply_reduce_fusion.1
  22.9 106.7 %all-reduce = (f32[2,16,16]{2,1,0:T(8,128)S(1)}, f32[2,16,16]{2,1,0:T(8,128)S(1)}) all-reduce(f32[2,16,16]{2,1,0:T(8,128)S(1)} %multiply_reduce_fusion.1, f32[2,16,16]{2,1,0:T(8,128)S(1)} %multiply_reduce_fusion), channel_id=1, replica_groups=mesh['space'=8,'vel'=32] {'vel'}, use_global_device_ids=true, to_apply=%region_1.2 | all-reduce | flops 1024 | bytes 8192 | tf_op jit(solution)/shard_map/psum | solution.py:218
  129.8 1.4 copy-done.1
  131.2 0.6 copy-done.2
  131.8 0.9 select_select_fusion
  132.7 0.9 copy-done.6
  133.7 2.4 fusion.163
  136.1 0.9 fusion.229
  137.0 56.8 %psum.110 = f32[4,256]{1,0:T(4,128)S(1)} all-reduce(f32[4,256]{1,0:T(4,128)S(1)} %fusion.229), channel_id=1, replica_groups=mesh['space'=8,'vel'=32] {'vel'}, use_global_device_ids=true, to_apply=%region_4.5 | all-reduce | flops 1024 | bytes 8192 | tf_op jit(solution)/shard_map/psum | solution.py:149
  194.1 0.9 fusion.235
  195.3 53.0 %psum.111 = f32[4,256]{1,0:T(4,128)S(1)} all-reduce(f32[4,256]{1,0:T(4,128)S(1)} %pad_maximum_fusion.3), channel_id=1, replica_groups=mesh['space'=8,'vel'=32] {'vel'}, use_global_device_ids=true, to_apply=%region_9.10 | all-reduce | flops 1024 | bytes 8192 | tf_op jit(solution)/shard_map/psum | solution.py:167
  249.0 1.3 fusion.28
  250.2 0.9 fusion.228
  251.2 53.0 %psum.112 = f32[4,256]{1,0:T(4,128)S(1)} all-reduce(f32[4,256]{1,0:T(4,128)S(1)} %fusion.228), channel_id=1, replica_groups=mesh['space'=8,'vel'=32] {'vel'}, use_global_device_ids=true, to_apply=%region_10.11 | all-reduce | flops 1024 | bytes 8192 | tf_op jit(solution)/shard_map/psum | solution.py:149
  304.4 2.1 fusion.234
  306.9 53.0 %psum.113 = f32[4,256]{1,0:T(4,128)S(1)} all-reduce(f32[4,256]{1,0:T(4,128)S(1)} %pad_maximum_fusion.4), channel_id=1, replica_groups=mesh['space'=8,'vel'=32] {'vel'}, use_global_device_ids=true, to_apply=%region_15.16 | all-reduce | flops 1024 | bytes 8192 | tf_op jit(solution)/shard_map/psum | solution.py:167
  360.5 1.3 fusion.51
  361.8 0.9 fusion.227
  362.7 53.2 %psum.114 = f32[4,256]{1,0:T(4,128)S(1)} all-reduce(f32[4,256]{1,0:T(4,128)S(1)} %fusion.227), channel_id=1, replica_groups=mesh['space'=8,'vel'=32] {'vel'}, use_global_device_ids=true, to_apply=%region_16.17 | all-reduce | flops 1024 | bytes 8192 | tf_op jit(solution)/shard_map/psum | solution.py:149
  416.2 2.1 fusion.233
  418.6 53.0 %psum.115 = f32[4,256]{1,0:T(4,128)S(1)} all-reduce(f32[4,256]{1,0:T(4,128)S(1)} %pad_maximum_fusion.5), channel_id=1, replica_groups=mesh['space'=8,'vel'=32] {'vel'}, use_global_device_ids=true, to_apply=%region_21.22 | all-reduce | flops 1024 | bytes 8192 | tf_op jit(solution)/shard_map/psum | solution.py:167
  472.2 1.3 fusion.74
  473.5 1.2 fusion.245
  474.7 1.3 collective-permute-start.2
  476.0 5.0 collective-permute-start.3
  481.3 113.0 %psum.116 = f32[2,16,16]{2,1,0:T(8,128)S(1)} all-reduce(f32[2,16,16]{2,1,0:T(8,128)S(1)} %fusion.4), channel_id=1, replica_groups=mesh['space'=8,'vel'=32] {'vel'}, use_global_device_ids=true, to_apply=%region_23.24 | all-reduce | flops 512 | bytes 4096 | tf_op jit(solution)/shard_map/psum | solution.py:218
  594.6 1.3 copy-done.3
  596.0 0.9 fusion.5
  597.1 5.7 fusion.152
  602.9 0.9 fusion.226
  603.8 56.8 %psum.117 = f32[4,256]{1,0:T(4,128)S(1)} all-reduce(f32[4,256]{1,0:T(4,128)S(1)} %fusion.226), channel_id=1, replica_groups=mesh['space'=8,'vel'=32] {'vel'}, use_global_device_ids=true, to_apply=%region_24.25 | all-reduce | flops 1024 | bytes 8192 | tf_op jit(solution)/shard_map/psum | solution.py:149
  660.8 0.9 fusion.232
  662.1 53.0 %psum.118 = f32[4,256]{1,0:T(4,128)S(1)} all-reduce(f32[4,256]{1,0:T(4,128)S(1)} %pad_maximum_fusion.6), channel_id=1, replica_groups=mesh['space'=8,'vel'=32] {'vel'}, use_global_device_ids=true, to_apply=%region_29.30 | all-reduce | flops 1024 | bytes 8192 | tf_op jit(solution)/shard_map/psum | solution.py:167
  715.7 1.3 fusion.97
  717.0 0.9 fusion.225
  717.9 53.0 %psum.119 = f32[4,256]{1,0:T(4,128)S(1)} all-reduce(f32[4,256]{1,0:T(4,128)S(1)} %fusion.225), channel_id=1, replica_groups=mesh['space'=8,'vel'=32] {'vel'}, use_global_device_ids=true, to_apply=%region_30.31 | all-reduce | flops 1024 | bytes 8192 | tf_op jit(solution)/shard_map/psum | solution.py:149
  771.2 2.1 fusion.231
  773.6 53.2 %psum.120 = f32[4,256]{1,0:T(4,128)S(1)} all-reduce(f32[4,256]{1,0:T(4,128)S(1)} %pad_maximum_fusion.7), channel_id=1, replica_groups=mesh['space'=8,'vel'=32] {'vel'}, use_global_device_ids=true, to_apply=%region_35.36 | all-reduce | flops 1024 | bytes 8192 | tf_op jit(solution)/shard_map/psum | solution.py:167
  827.5 1.3 fusion.120
  828.8 0.9 fusion.224
  829.7 53.0 %psum.121 = f32[4,256]{1,0:T(4,128)S(1)} all-reduce(f32[4,256]{1,0:T(4,128)S(1)} %fusion.224), channel_id=1, replica_groups=mesh['space'=8,'vel'=32] {'vel'}, use_global_device_ids=true, to_apply=%region_36.37 | all-reduce | flops 1024 | bytes 8192 | tf_op jit(solution)/shard_map/psum | solution.py:149
  883.2 0.7 fusion.237
  884.1 2.1 fusion.230
  886.5 53.0 %psum.122 = f32[4,256]{1,0:T(4,128)S(1)} all-reduce(f32[4,256]{1,0:T(4,128)S(1)} %pad_maximum_fusion.8), channel_id=1, replica_groups=mesh['space'=8,'vel'=32] {'vel'}, use_global_device_ids=true, to_apply=%region_41.42 | all-reduce | flops 1024 | bytes 8192 | tf_op jit(solution)/shard_map/psum | solution.py:167
  939.5 0.7 slice_reduce_fusion.2
  940.3 0.7 slice.445
  941.6 2.0 fusion.143
  (208 shorter events, 9.8 us)
Async XLA Ops:
  0.6 15.8 %copy-start = (f32[1,16,16,1024]{3,2,1,0:T(8,128)S(1)}, f32[1,16,16,1024]{3,2,1,0:T(8,128)}, u32[]{:S(2)}) copy-start(f32[1,16,16,1024]{3,2,1,0:T(8,128)} %param.4) | copy-start | bytes 3145732
  0.6 132.1 %collective-permute-start = (f32[1,16,16,1024]{3,2,1,0:T(8,128)}, f32[1,16,16,1024]{3,2,1,0:T(8,128)S(1)}, u32[]{:S(2)}, u32[]{:S(2)}) collective-permute-start(f32[1,16,16,1024]{3,2,1,0:T(8,128)} %param.4), channel_id=1, source_target_pairs={{0,32},{32,64},{64,96},{96,128},{128,160},{160,192},{192,224},{1,3... | collective-permute-start | bytes 3145736 | tf_op jit(solution)/shard_map/ppermute | solution.py:26
  2.1 130.7 %collective-permute-start.1 = (f32[1,16,16,1024]{3,2,1,0:T(8,128)}, f32[1,16,16,1024]{3,2,1,0:T(8,128)}, u32[]{:S(2)}, u32[]{:S(2)}) collective-permute-start(f32[1,16,16,1024]{3,2,1,0:T(8,128)} %param.4), channel_id=1, source_target_pairs={{32,0},{64,32},{96,64},{128,96},{160,128},{192,160},{224,192},{33,... | collective-permute-start | bytes 3145736 | tf_op jit(solution)/shard_map/ppermute | solution.py:28
  16.5 1.3 copy-start.25
  17.7 1.3 copy-start.26
  20.3 113.4 %copy-start.7 = (f32[1024]{0:T(1024)}, f32[1024]{0:T(1024)S(1)}, u32[]{:S(2)}) copy-start(f32[1024]{0:T(1024)S(1)} %get-tuple-element.130) | copy-start | bytes 12292
  20.3 113.4 %copy-start.9 = (f32[1024]{0:T(1024)}, f32[1024]{0:T(1024)S(1)}, u32[]{:S(2)}) copy-start(f32[1024]{0:T(1024)S(1)} %get-tuple-element.184) | copy-start | bytes 12292
  20.3 109.5 %copy-start.21 = (f32[1024]{0:T(1024)}, f32[1024]{0:T(1024)S(1)}, u32[]{:S(2)}) copy-start(f32[1024]{0:T(1024)S(1)} %get-tuple-element.180) | copy-start | bytes 12292
  20.3 113.4 %copy-start.11 = (f32[1024]{0:T(1024)}, f32[1024]{0:T(1024)S(1)}, u32[]{:S(2)}) copy-start(f32[1024]{0:T(1024)S(1)} %get-tuple-element.179) | copy-start | bytes 12292
  20.3 113.4 %copy-start.13 = (f32[1024]{0:T(1024)}, f32[1024]{0:T(1024)S(1)}, u32[]{:S(2)}) copy-start(f32[1024]{0:T(1024)S(1)} %get-tuple-element.181) | copy-start | bytes 12292
  20.4 113.3 %copy-start.15 = (f32[1024]{0:T(1024)}, f32[1024]{0:T(1024)S(1)}, u32[]{:S(2)}) copy-start(f32[1024]{0:T(1024)S(1)} %get-tuple-element.182) | copy-start | bytes 12292
  22.9 107.0 %copy-start.17 = (pred[2,16,16]{2,1,0:T(8,128)(4,1)S(1)}, pred[2,16,16]{2,1,0:T(8,128)(4,1)}, u32[]{:S(2)}) copy-start(pred[2,16,16]{2,1,0:T(8,128)(4,1)} %get-tuple-element.132) | copy-start | bytes 1540
  22.9 107.0 %copy-start.19 = (pred[2,16,16]{2,1,0:T(8,128)(4,1)S(1)}, pred[2,16,16]{2,1,0:T(8,128)(4,1)}, u32[]{:S(2)}) copy-start(pred[2,16,16]{2,1,0:T(8,128)(4,1)} %get-tuple-element.133) | copy-start | bytes 1540
  129.6 232.2 %copy-start.23 = (f32[4]{0:T(128)}, f32[4]{0:T(128)S(1)}, u32[]{:S(2)}) copy-start(f32[4]{0:T(128)S(1)} %pad.34.clone) | copy-start | bytes 52
  129.6 1.6 copy-start.1
  129.6 2.2 copy-start.2
  131.8 1.9 copy-start.4
  132.7 1.0 copy-start.6
  474.7 122.2 %collective-permute-start.2 = (f32[1,16,16,1024]{3,2,1,0:T(8,128)S(1)}, f32[1,16,16,1024]{3,2,1,0:T(8,128)}, u32[]{:S(2)}, u32[]{:S(2)}) collective-permute-start(f32[1,16,16,1024]{3,2,1,0:T(8,128)S(1)} %fusion.74), channel_id=1, source_target_pairs={{0,32},{32,64},{64,96},{96,128},{128,160},{160,192},{192,224},{1,3... | collective-permute-start | bytes 3145736 | tf_op jit(solution)/shard_map/ppermute | solution.py:26
  476.0 120.9 %collective-permute-start.3 = (f32[1,16,16,1024]{3,2,1,0:T(8,128)S(1)}, f32[1,16,16,1024]{3,2,1,0:T(8,128)}, u32[]{:S(2)}, u32[]{:S(2)}) collective-permute-start(f32[1,16,16,1024]{3,2,1,0:T(8,128)S(1)} %fusion.74), channel_id=1, source_target_pairs={{32,0},{64,32},{96,64},{128,96},{160,128},{192,160},{224,192},{33,... | collective-permute-start | bytes 3145736 | tf_op jit(solution)/shard_map/ppermute | solution.py:28
  594.3 1.6 copy-start.3
  594.3 1.6 copy-start.18
  594.3 1.6 copy-start.20
  594.3 1.6 copy-start.22
  595.9 1.2 copy-start.5
  595.9 1.2 copy-start.8
  595.9 1.2 copy-start.10
  595.9 1.2 copy-start.12
  595.9 1.2 copy-start.14
  596.0 1.2 copy-start.16
  597.1 5.7 copy-start.24
where the time goes:
time: 944 us
  blocking collectives  864 us (92%)
  other arithmetic  41.6 us (4%)
  local copies, waits for them, and re-layouts  18.9 us (2%)
  starting transfers between devices  12.7 us (1%)
    psum x6, blocking collectives, moment_fields(): first_sum = lax.psum(partial_value, 'vel') / velocity_total  326 us
    psum x6, blocking collectives, moment_fields(): second = lax.psum(second, 'vel') / velocity_total  318 us
    psum x2, blocking collectives, body(): leaving, entering = lax.psum((leaving_part, entering_part), 'vel')  220 us
  transfers between devices with their start and end apart: 4, of which 0 were waited for; matrix products, arithmetic and copies ran while one was open for 2% of the time, Pallas kernels for 0%

commit v1 on v0

--- a/solution.py
+++ b/solution.py
@@ -146,7 +146,7 @@
     partial_value = jnp.einsum(
         "cv,vk->kc", flattened, moment_table[:, :4], precision=lax.Precision.HIGHEST
     )
-    first_sum = lax.psum(partial_value, "vel") / velocity_total
+    first_sum = jnp.sum(lax.all_gather(partial_value, "vel"), axis=0) / velocity_total
     particle_concentration = first_sum[0]
     mean_motion_first_axis = first_sum[1] / particle_concentration
     mean_motion_second_axis = first_sum[2] / particle_concentration

time: 944 us -> 821 us (0.87)
  blocking collectives: 864 us -> 738 us
    psum x6 -> x0, blocking collectives: 326 us -> none  [moment_fields(): first_sum = lax.psum(partial_value, 'vel') / velocity_total]
    all_gather x0 -> x6, blocking collectives: none -> 203 us  [moment_fields(): lax.all_gather(partial_value, 'vel')]
where the time goes in v1:
time: 821 us; the launch traced here: 818 us
  blocking collectives  738 us (90%)
  other arithmetic  41.8 us (5%)
  local copies, waits for them, and re-layouts  18.9 us (2%)
  starting transfers between devices  12.7 us (2%)
    psum x6, blocking collectives, moment_fields(): second = lax.psum(second, 'vel') / velocity_total  315 us
    psum x2, blocking collectives, body(): leaving, entering = lax.psum((leaving_part, entering_part), 'vel')  220 us
    all_gather x6, blocking collectives, moment_fields(): lax.all_gather(partial_value, 'vel')  203 us
  transfers between devices with their start and end apart: 4, of which 0 were waited for; matrix products, arithmetic and copies ran while one was open for 2% of the time, Pallas kernels for 0%

profile of v1, /device:TPU:23, one launch (start us, length us, event | category | flops | bytes accessed | tf_op | source)
XLA Modules:
  0.0 818.2 jit_solution(700167760413803789)
XLA Ops:
  0.6 1.4 collective-permute-start
  2.1 5.0 collective-permute-start.1
  7.1 0.8 negate_select_fusion
  7.8 0.8 negate_select_fusion.1
  8.6 0.7 negate_select_fusion.3
  9.3 0.7 negate_select_fusion.6
  10.0 0.7 broadcast_compare_fusion
  10.7 0.7 broadcast_compare_fusion.1
  11.4 0.6 fusion.186
  12.1 0.7 fusion.187
  12.8 0.7 sign_compare_fusion
  13.5 0.7 sign_compare_fusion.1
  14.1 2.3 constant_dynamic-update-slice_fusion.1
  16.5 1.2 fusion.243
  17.8 1.1 constant_dynamic-update-slice_fusion
  19.5 0.8 broadcast_maximum_fusion.2
  20.4 0.7 multiply_reduce_fusion
  21.0 1.8 multiply_reduce_fusion.1
  22.9 106.7 %all-reduce = (f32[2,16,16]{2,1,0:T(8,128)S(1)}, f32[2,16,16]{2,1,0:T(8,128)S(1)}) all-reduce(f32[2,16,16]{2,1,0:T(8,128)S(1)} %multiply_reduce_fusion.1, f32[2,16,16]{2,1,0:T(8,128)S(1)} %multiply_reduce_fusion), channel_id=1, replica_groups=mesh['space'=8,'vel'=32] {'vel'}, use_global_device_ids=true, to_apply=%region_1.2 | all-reduce | flops 1024 | bytes 8192 | tf_op jit(solution)/shard_map/psum | solution.py:218
  129.8 1.4 copy-done.1
  131.2 0.6 copy-done.2
  131.8 0.9 select_select_fusion
  132.7 0.9 copy-done.6
  133.7 2.4 fusion.163
  136.1 0.9 convolution_bitcast_fusion.5
  137.0 35.0 %all-gather.6 = f32[32,4,256]{2,1,0:T(4,128)S(1)} all-gather(f32[1,4,256]{2,1,0:T(4,128)S(1)} %convolution_bitcast_fusion.5), channel_id=2, replica_groups=mesh['space'=8,'vel'=32] {'vel'}, dimensions={0}, use_global_device_ids=true | all-gather | bytes 135168 | tf_op jit(solution)/shard_map/all_gather | solution.py:149
  172.3 0.9 fusion.229
  173.6 52.5 %psum.68 = f32[4,256]{1,0:T(4,128)S(1)} all-reduce(f32[4,256]{1,0:T(4,128)S(1)} %pad_maximum_fusion.3), channel_id=1, replica_groups=mesh['space'=8,'vel'=32] {'vel'}, use_global_device_ids=true, to_apply=%region_9.10 | all-reduce | flops 1024 | bytes 8192 | tf_op jit(solution)/shard_map/psum | solution.py:167
  226.8 1.3 fusion.28
  228.0 0.9 convolution_bitcast_fusion.4
  228.9 33.2 %all-gather.7 = f32[32,4,256]{2,1,0:T(4,128)S(1)} all-gather(f32[1,4,256]{2,1,0:T(4,128)S(1)} %convolution_bitcast_fusion.4), channel_id=3, replica_groups=mesh['space'=8,'vel'=32] {'vel'}, dimensions={0}, use_global_device_ids=true | all-gather | bytes 135168 | tf_op jit(solution)/shard_map/all_gather | solution.py:149
  262.4 2.1 fusion.228
  264.9 52.7 %psum.69 = f32[4,256]{1,0:T(4,128)S(1)} all-reduce(f32[4,256]{1,0:T(4,128)S(1)} %pad_maximum_fusion.4), channel_id=1, replica_groups=mesh['space'=8,'vel'=32] {'vel'}, use_global_device_ids=true, to_apply=%region_15.16 | all-reduce | flops 1024 | bytes 8192 | tf_op jit(solution)/shard_map/psum | solution.py:167
  318.2 1.3 fusion.51
  319.5 0.9 convolution_bitcast_fusion.3
  320.4 33.2 %all-gather.8 = f32[32,4,256]{2,1,0:T(4,128)S(1)} all-gather(f32[1,4,256]{2,1,0:T(4,128)S(1)} %convolution_bitcast_fusion.3), channel_id=4, replica_groups=mesh['space'=8,'vel'=32] {'vel'}, dimensions={0}, use_global_device_ids=true | all-gather | bytes 135168 | tf_op jit(solution)/shard_map/all_gather | solution.py:149
  353.9 2.1 fusion.227
  356.4 52.5 %psum.70 = f32[4,256]{1,0:T(4,128)S(1)} all-reduce(f32[4,256]{1,0:T(4,128)S(1)} %pad_maximum_fusion.5), channel_id=1, replica_groups=mesh['space'=8,'vel'=32] {'vel'}, use_global_device_ids=true, to_apply=%region_21.22 | all-reduce | flops 1024 | bytes 8192 | tf_op jit(solution)/shard_map/psum | solution.py:167
  409.5 1.3 fusion.74
  410.8 1.2 fusion.239
  412.0 1.3 collective-permute-start.2
  413.3 5.0 collective-permute-start.3
  418.6 113.0 %psum.71 = f32[2,16,16]{2,1,0:T(8,128)S(1)} all-reduce(f32[2,16,16]{2,1,0:T(8,128)S(1)} %fusion.4), channel_id=1, replica_groups=mesh['space'=8,'vel'=32] {'vel'}, use_global_device_ids=true, to_apply=%region_23.24 | all-reduce | flops 512 | bytes 4096 | tf_op jit(solution)/shard_map/psum | solution.py:218
  531.9 1.3 copy-done.3
  533.3 0.9 fusion.5
  534.5 5.7 fusion.152
  540.2 0.9 convolution_bitcast_fusion.2
  541.1 35.0 %all-gather.9 = f32[32,4,256]{2,1,0:T(4,128)S(1)} all-gather(f32[1,4,256]{2,1,0:T(4,128)S(1)} %convolution_bitcast_fusion.2), channel_id=5, replica_groups=mesh['space'=8,'vel'=32] {'vel'}, dimensions={0}, use_global_device_ids=true | all-gather | bytes 135168 | tf_op jit(solution)/shard_map/all_gather | solution.py:149
  576.4 0.9 fusion.226
  577.7 52.5 %psum.72 = f32[4,256]{1,0:T(4,128)S(1)} all-reduce(f32[4,256]{1,0:T(4,128)S(1)} %pad_maximum_fusion.6), channel_id=1, replica_groups=mesh['space'=8,'vel'=32] {'vel'}, use_global_device_ids=true, to_apply=%region_29.30 | all-reduce | flops 1024 | bytes 8192 | tf_op jit(solution)/shard_map/psum | solution.py:167
  630.8 1.3 fusion.97
  632.1 0.9 convolution_bitcast_fusion.1
  633.0 33.4 %all-gather.10 = f32[32,4,256]{2,1,0:T(4,128)S(1)} all-gather(f32[1,4,256]{2,1,0:T(4,128)S(1)} %convolution_bitcast_fusion.1), channel_id=6, replica_groups=mesh['space'=8,'vel'=32] {'vel'}, dimensions={0}, use_global_device_ids=true | all-gather | bytes 135168 | tf_op jit(solution)/shard_map/all_gather | solution.py:149
  666.7 2.1 fusion.225
  669.2 52.5 %psum.73 = f32[4,256]{1,0:T(4,128)S(1)} all-reduce(f32[4,256]{1,0:T(4,128)S(1)} %pad_maximum_fusion.7), channel_id=1, replica_groups=mesh['space'=8,'vel'=32] {'vel'}, use_global_device_ids=true, to_apply=%region_35.36 | all-reduce | flops 1024 | bytes 8192 | tf_op jit(solution)/shard_map/psum | solution.py:167
  722.3 1.3 fusion.120
  723.6 0.9 convolution_bitcast_fusion
  724.5 33.2 %all-gather.11 = f32[32,4,256]{2,1,0:T(4,128)S(1)} all-gather(f32[1,4,256]{2,1,0:T(4,128)S(1)} %convolution_bitcast_fusion), channel_id=7, replica_groups=mesh['space'=8,'vel'=32] {'vel'}, dimensions={0}, use_global_device_ids=true | all-gather | bytes 135168 | tf_op jit(solution)/shard_map/all_gather | solution.py:149
  758.3 0.7 fusion.231
  759.2 2.1 fusion.224
  761.6 52.5 %psum.74 = f32[4,256]{1,0:T(4,128)S(1)} all-reduce(f32[4,256]{1,0:T(4,128)S(1)} %pad_maximum_fusion.8), channel_id=1, replica_groups=mesh['space'=8,'vel'=32] {'vel'}, use_global_device_ids=true, to_apply=%region_41.42 | all-reduce | flops 1024 | bytes 8192 | tf_op jit(solution)/shard_map/psum | solution.py:167
  814.2 0.7 slice_reduce_fusion.2
  814.9 0.7 slice.445
  816.2 2.0 fusion.143
  (214 shorter events, 10.1 us)
Async XLA Ops:
  0.6 15.8 %copy-start = (f32[1,16,16,1024]{3,2,1,0:T(8,128)S(1)}, f32[1,16,16,1024]{3,2,1,0:T(8,128)}, u32[]{:S(2)}) copy-start(f32[1,16,16,1024]{3,2,1,0:T(8,128)} %param.4) | copy-start | bytes 3145732
  0.6 132.1 %collective-permute-start = (f32[1,16,16,1024]{3,2,1,0:T(8,128)}, f32[1,16,16,1024]{3,2,1,0:T(8,128)S(1)}, u32[]{:S(2)}, u32[]{:S(2)}) collective-permute-start(f32[1,16,16,1024]{3,2,1,0:T(8,128)} %param.4), channel_id=1, source_target_pairs={{0,32},{32,64},{64,96},{96,128},{128,160},{160,192},{192,224},{1,3... | collective-permute-start | bytes 3145736 | tf_op jit(solution)/shard_map/ppermute | solution.py:26
  2.1 130.7 %collective-permute-start.1 = (f32[1,16,16,1024]{3,2,1,0:T(8,128)}, f32[1,16,16,1024]{3,2,1,0:T(8,128)}, u32[]{:S(2)}, u32[]{:S(2)}) collective-permute-start(f32[1,16,16,1024]{3,2,1,0:T(8,128)} %param.4), channel_id=1, source_target_pairs={{32,0},{64,32},{96,64},{128,96},{160,128},{192,160},{224,192},{33,... | collective-permute-start | bytes 3145736 | tf_op jit(solution)/shard_map/ppermute | solution.py:28
  16.5 1.3 copy-start.25
  17.7 1.3 copy-start.26
  20.3 113.4 %copy-start.7 = (f32[1024]{0:T(1024)}, f32[1024]{0:T(1024)S(1)}, u32[]{:S(2)}) copy-start(f32[1024]{0:T(1024)S(1)} %get-tuple-element.126) | copy-start | bytes 12292
  20.3 113.4 %copy-start.9 = (f32[1024]{0:T(1024)}, f32[1024]{0:T(1024)S(1)}, u32[]{:S(2)}) copy-start(f32[1024]{0:T(1024)S(1)} %get-tuple-element.180) | copy-start | bytes 12292
  20.3 109.5 %copy-start.21 = (f32[1024]{0:T(1024)}, f32[1024]{0:T(1024)S(1)}, u32[]{:S(2)}) copy-start(f32[1024]{0:T(1024)S(1)} %get-tuple-element.176) | copy-start | bytes 12292
  20.3 113.4 %copy-start.11 = (f32[1024]{0:T(1024)}, f32[1024]{0:T(1024)S(1)}, u32[]{:S(2)}) copy-start(f32[1024]{0:T(1024)S(1)} %get-tuple-element.175) | copy-start | bytes 12292
  20.3 113.4 %copy-start.13 = (f32[1024]{0:T(1024)}, f32[1024]{0:T(1024)S(1)}, u32[]{:S(2)}) copy-start(f32[1024]{0:T(1024)S(1)} %get-tuple-element.177) | copy-start | bytes 12292
  20.4 113.3 %copy-start.15 = (f32[1024]{0:T(1024)}, f32[1024]{0:T(1024)S(1)}, u32[]{:S(2)}) copy-start(f32[1024]{0:T(1024)S(1)} %get-tuple-element.178) | copy-start | bytes 12292
  22.9 107.0 %copy-start.17 = (pred[2,16,16]{2,1,0:T(8,128)(4,1)S(1)}, pred[2,16,16]{2,1,0:T(8,128)(4,1)}, u32[]{:S(2)}) copy-start(pred[2,16,16]{2,1,0:T(8,128)(4,1)} %get-tuple-element.128) | copy-start | bytes 1540
  22.9 107.0 %copy-start.19 = (pred[2,16,16]{2,1,0:T(8,128)(4,1)S(1)}, pred[2,16,16]{2,1,0:T(8,128)(4,1)}, u32[]{:S(2)}) copy-start(pred[2,16,16]{2,1,0:T(8,128)(4,1)} %get-tuple-element.129) | copy-start | bytes 1540
  129.6 189.9 %copy-start.23 = (f32[4]{0:T(128)}, f32[4]{0:T(128)S(1)}, u32[]{:S(2)}) copy-start(f32[4]{0:T(128)S(1)} %pad.34.clone) | copy-start | bytes 52
  129.6 1.6 copy-start.1
  129.6 2.2 copy-start.2
  131.8 1.9 copy-start.4
  132.7 1.0 copy-start.6
  412.0 122.2 %collective-permute-start.2 = (f32[1,16,16,1024]{3,2,1,0:T(8,128)S(1)}, f32[1,16,16,1024]{3,2,1,0:T(8,128)}, u32[]{:S(2)}, u32[]{:S(2)}) collective-permute-start(f32[1,16,16,1024]{3,2,1,0:T(8,128)S(1)} %fusion.74), channel_id=1, source_target_pairs={{0,32},{32,64},{64,96},{96,128},{128,160},{160,192},{192,224},{1,3... | collective-permute-start | bytes 3145736 | tf_op jit(solution)/shard_map/ppermute | solution.py:26
  413.3 120.9 %collective-permute-start.3 = (f32[1,16,16,1024]{3,2,1,0:T(8,128)S(1)}, f32[1,16,16,1024]{3,2,1,0:T(8,128)}, u32[]{:S(2)}, u32[]{:S(2)}) collective-permute-start(f32[1,16,16,1024]{3,2,1,0:T(8,128)S(1)} %fusion.74), channel_id=1, source_target_pairs={{32,0},{64,32},{96,64},{128,96},{160,128},{192,160},{224,192},{33,... | collective-permute-start | bytes 3145736 | tf_op jit(solution)/shard_map/ppermute | solution.py:28
  531.6 1.6 copy-start.3
  531.6 1.6 copy-start.18
  531.6 1.6 copy-start.20
  531.6 1.6 copy-start.22
  533.2 1.2 copy-start.5
  533.2 1.2 copy-start.8
  533.2 1.2 copy-start.10
  533.3 1.2 copy-start.12
  533.3 1.2 copy-start.14
  533.3 1.2 copy-start.16
  534.5 5.7 copy-start.24
